TPU v7x, 32 devices: a whole 2x2x4 slice. The times are simulated.
32 devices in a mesh: dp: 8 (over y, x, core), tensor: 4 (over z).
Axes of the slice: x: 2, y: 2, z: 4, core: 2. Of those that a mesh axis runs over, the one named last changes fastest.
Arguments:
- tokens: bfloat16 [4096, 2304], P(('dp', 'tensor')), may hold values from -6 to 6
- cotangent: bfloat16 [4096, 4096], P('dp', 'tensor'), may hold values from -6 to 6
- pre_gain: float32 [2304], replicated, may hold values from 0.25 to 1.75
- w_query: bfloat16 [2304, 4096], P('dp', 'tensor'), may hold values from -0.375 to 0.375
- key_weight: bfloat16 [2304, 2048], P('dp', 'tensor'), may hold values from -0.375 to 0.375
- value_weight: bfloat16 [2304, 2048], P('dp', 'tensor'), may hold values from -0.125 to 0.125
Outputs:
- attended: bfloat16 [4096, 4096], P('dp', 'tensor')
- grad_tokens: bfloat16 [4096, 2304], P(('dp', 'tensor'))
- grad_query: float32 [2304, 4096], P('dp', 'tensor')
- grad_key: float32 [2304, 2048], P('dp', 'tensor')
- grad_value: float32 [2304, 2048], P('dp', 'tensor')
- grad_pre_gain: float32 [2304], replicated
All inputs are finite; a program needn't handle non-finite values.
Results may differ from a plain program's by a relative error of at most 0.019.
The roundings to bfloat16 on the way count: a program that leaves them out, or rounds other values in their place, can miss the bound.
Values may be sent and summed in bfloat16 or wider, within the bound.
A program may use at most 192 MiB of HBM per device.

v0:
```python
import jax
import jax.numpy as jnp
from jax import lax
from jax.sharding import PartitionSpec as P

HEAD_SIZE = 128
SEQ_LEN = 64
EPS = 1e-06
CAP = 50.0
BASE = 10000.0
query_scalar = 144.0


def rotary_tables(segment_length, half):
    places = jnp.arange(segment_length, dtype=jnp.float32)[:, None]
    freqs = BASE ** (-jnp.arange(half, dtype=jnp.float32) / half)
    angles = places * freqs[None, :]
    return (jnp.cos(angles)[:, None, :], jnp.sin(angles)[:, None, :])


def rotate(values, cosine_table, sine_table):
    half = values.shape[-1] // 2
    first, second = (values[..., :half], values[..., half:])
    return jnp.concatenate(
        [first * cosine_table - second * sine_table, second * cosine_table + first * sine_table], -1
    )


def inverse_rotation(values, cosine_table, sine_table):
    half = values.shape[-1] // 2
    first, second = (values[..., :half], values[..., half:])
    return jnp.concatenate(
        [first * cosine_table + second * sine_table, second * cosine_table - first * sine_table], -1
    )


def attend_forward(query, key, value):
    repeat = query.shape[1] // key.shape[1]
    keys = jnp.repeat(key, repeat, axis=1)
    values = jnp.repeat(value, repeat, axis=1)
    factor = query_scalar ** (-0.5)
    raw = jnp.einsum("qhd,khd->hqk", query, keys, preferred_element_type=jnp.float32) * factor
    bent = jnp.tanh(raw / CAP)
    capped = CAP * bent
    segment_length = query.shape[0]
    causal = jnp.arange(segment_length)[None, :] <= jnp.arange(segment_length)[:, None]
    raised = jnp.where(causal[None], jnp.exp(capped), 0.0)
    weights = raised / jnp.sum(raised, -1, keepdims=True)
    probs = weights.astype(jnp.bfloat16)
    attended = jnp.einsum("hqk,khd->qhd", probs, values, preferred_element_type=jnp.float32).astype(
        jnp.bfloat16
    )
    return (attended, weights, probs, bent)


def attend_backward(d_attended, query, key, value, weights, probs, bent):
    repeat = query.shape[1] // key.shape[1]
    keys = jnp.repeat(key, repeat, axis=1)
    values = jnp.repeat(value, repeat, axis=1)
    factor = query_scalar ** (-0.5)
    d_probs = jnp.einsum("qhd,khd->hqk", d_attended, values, preferred_element_type=jnp.float32)
    d_capped = weights * (d_probs - jnp.sum(weights * d_probs, -1, keepdims=True))
    d_scores = (d_capped * (1.0 - bent * bent) * factor).astype(jnp.bfloat16)
    query_back = jnp.einsum("hqk,khd->qhd", d_scores, keys, preferred_element_type=jnp.float32)
    key_heads = jnp.einsum("hqk,qhd->khd", d_scores, query, preferred_element_type=jnp.float32)
    value_heads = jnp.einsum("hqk,qhd->khd", probs, d_attended, preferred_element_type=jnp.float32)
    segment_length, heads, width = query.shape
    key_rotated_back = key_heads.reshape(segment_length, heads // repeat, repeat, width).sum(2)
    value_returned = value_heads.reshape(segment_length, heads // repeat, repeat, width).sum(2)
    return (query_back, key_rotated_back, value_returned)


def segment_pass(query, key, value, d_attended):
    attended, weights, probs, bent = attend_forward(query, key, value)
    query_back, key_rotated_back, value_returned = attend_backward(
        d_attended, query, key, value, weights, probs, bent
    )
    return (attended, query_back, key_rotated_back, value_returned)


def per_device(tokens, cotangent, pre_gain, w_query, key_weight, value_weight):
    contract_first = (((0,), (0,)), ((), ()))
    contract_last = (((1,), (1,)), ((), ()))
    rows_f = tokens.astype(jnp.float32)
    inv_one = lax.rsqrt(jnp.mean(rows_f * rows_f, -1, keepdims=True) + EPS)
    unit_one = rows_f * inv_one
    normed_input = (unit_one * pre_gain).astype(jnp.bfloat16)
    gathered = lax.all_gather(normed_input, "tensor", axis=0, tiled=True)
    segment_length = gathered.shape[0]
    token_span = SEQ_LEN
    pieces_count = segment_length // token_span
    heads_query = w_query.shape[1] // HEAD_SIZE
    heads_key = key_weight.shape[1] // HEAD_SIZE
    pieces = (
        lax.all_gather(w_query, "dp", axis=0, tiled=True),
        lax.all_gather(key_weight, "dp", axis=0, tiled=True),
        lax.all_gather(value_weight, "dp", axis=0, tiled=True),
    )
    query_raw, key_unrotated, value_projected = tuple(
        (jnp.dot(gathered, piece, preferred_element_type=jnp.float32) for piece in pieces)
    )
    cosine_table, sine_table = rotary_tables(token_span, HEAD_SIZE // 2)
    query = rotate(
        query_raw.reshape(pieces_count, token_span, heads_query, HEAD_SIZE),
        cosine_table,
        sine_table,
    ).astype(jnp.bfloat16)
    key = rotate(
        key_unrotated.reshape(pieces_count, token_span, heads_key, HEAD_SIZE),
        cosine_table,
        sine_table,
    ).astype(jnp.bfloat16)
    value = value_projected.reshape(pieces_count, token_span, heads_key, HEAD_SIZE).astype(
        jnp.bfloat16
    )
    d_attended = cotangent.reshape(pieces_count, token_span, heads_query, HEAD_SIZE)
    attended, query_back, key_rotated_back, value_returned = jax.vmap(segment_pass)(
        query, key, value, d_attended
    )
    attended_flat = attended.reshape(segment_length, heads_query * HEAD_SIZE)
    d_query = (
        inverse_rotation(query_back, cosine_table, sine_table)
        .astype(jnp.bfloat16)
        .reshape(segment_length, heads_query * HEAD_SIZE)
    )
    key_gradient = (
        inverse_rotation(key_rotated_back, cosine_table, sine_table)
        .astype(jnp.bfloat16)
        .reshape(segment_length, heads_key * HEAD_SIZE)
    )
    value_gradient = value_returned.astype(jnp.bfloat16).reshape(
        segment_length, heads_key * HEAD_SIZE
    )
    back_query, back_key, back_value = (
        lax.all_gather(w_query, "dp", axis=0, tiled=True),
        lax.all_gather(key_weight, "dp", axis=0, tiled=True),
        lax.all_gather(value_weight, "dp", axis=0, tiled=True),
    )
    joined = jnp.concatenate([d_query, key_gradient, value_gradient], 1)
    block = gathered
    grads = lax.psum_scatter(
        lax.dot_general(block, joined, contract_first, preferred_element_type=jnp.float32).astype(
            jnp.bfloat16
        ),
        "dp",
        scatter_dimension=0,
        tiled=True,
    ).astype(jnp.float32)
    width_query = w_query.shape[1]
    width_key = key_weight.shape[1]
    grad_query = grads[:, :width_query]
    grad_key = grads[:, width_query : width_query + width_key]
    grad_value = grads[:, width_query + width_key :]
    total = jnp.zeros((tokens.shape[0] * lax.axis_size("tensor"), gathered.shape[1]), jnp.float32)
    for grad_part, weight in (
        (d_query, back_query),
        (key_gradient, back_key),
        (value_gradient, back_value),
    ):
        block = grad_part
        total = total + lax.dot_general(
            block, weight, contract_last, preferred_element_type=jnp.float32
        )
    d_normed = lax.psum_scatter(
        total.astype(jnp.bfloat16), "tensor", scatter_dimension=0, tiled=True
    ).astype(jnp.float32)
    pre_part = jnp.sum(d_normed * unit_one, 0)
    scaled_in = d_normed * pre_gain
    grad_tokens = (
        inv_one * (scaled_in - unit_one * jnp.mean(scaled_in * unit_one, -1, keepdims=True))
    ).astype(jnp.bfloat16)
    grad_pre = lax.psum(pre_part, ("dp", "tensor"))
    return (attended_flat, grad_tokens, grad_query, grad_key, grad_value, grad_pre)


def solution(mesh):
    placed = (
        P(("dp", "tensor"), None),
        P("dp", "tensor"),
        P(),
        P("dp", "tensor"),
        P("dp", "tensor"),
        P("dp", "tensor"),
    )
    return jax.shard_map(
        per_device,
        mesh=mesh,
        in_specs=placed,
        out_specs=(
            P("dp", "tensor"),
            P(("dp", "tensor"), None),
            P("dp", "tensor"),
            P("dp", "tensor"),
            P("dp", "tensor"),
            P(),
        ),
        check_vma=False,
    )
```

profile of v0, /device:TPU:0, one launch (start us, length us, event | category | flops | bytes accessed | tf_op | source)
XLA Modules:
  0.0 347.0 jit_solution(11530087274163512373)
XLA Ops:
  7.2 1.3 fusion.22
  8.6 2.1 fusion.20
  10.7 0.0 all-gather.7.cloned.1.call-start
  10.7 0.7 all-gather.7.cloned.1.call-update
  11.5 0.7 all-gather.11.cloned.1.call-update
  12.2 0.5 all-gather.9.cloned.1.call-update
  12.8 0.0 reduce-scatter.3.cloned.1.call-start
  12.8 0.3 copy.62
  13.1 0.1 fusion.34
  13.3 50.3 %all-gather.5.cloned.1.call-done = bf16[512,2304]{1,0:T(8,128)(2,1)} async-done(((bf16[128,2304]{1,0:T(8,128)(2,1)}), bf16[512,2304]{1,0:T(8,128)(2,1)}) %all-gather.5.cloned.1.call-update) | async-done | bytes 2359312 | tf_op jit(solution)/shard_map/all_gather | solution.py:88
  63.6 29.6 %all-gather.7.cloned.1.call-done = bf16[2304,512]{1,0:T(8,128)(2,1)} async-done(((bf16[288,512]{1,0:T(8,128)(2,1)}), bf16[2304,512]{1,0:T(8,128)(2,1)}) %all-gather.7.cloned.1.call-update) | async-done | bytes 2359312 | tf_op jit(solution)/shard_map/all_gather | solution.py:97
  93.1 3.8 %convolution_convert_fusion.2 = bf16[512,512]{1,0:T(8,128)(2,1)S(1)} fusion(bf16[512,2304]{1,0:T(8,128)(2,1)} %all-gather.5.cloned.1.call-done, bf16[2304,512]{1,0:T(8,128)(2,1)} %all-gather.7.cloned.1.call-done), kind=kOutput, calls=%fused_computation.36 | convolution fusion | flops 1208221696 | bytes 5242880 | tf_op jit(solution)/shard_map/dot_general | solution.py:100
  96.9 0.1 convert_element_type.61
  97.0 0.1 copy.41
  97.1 26.8 %all-gather.11.cloned.1.call-done = bf16[2304,512]{1,0:T(8,128)(2,1)} async-done(((bf16[288,512]{1,0:T(8,128)(2,1)}), bf16[2304,512]{1,0:T(8,128)(2,1)}) %all-gather.11.cloned.1.call-update) | async-done | bytes 2359312 | tf_op jit(solution)/shard_map/all_gather | solution.py:96
  123.9 4.7 %fusion.56 = f32[512,512]{1,0:T(8,128)} fusion(bf16[512,2304]{1,0:T(8,128)(2,1)} %all-gather.5.cloned.1.call-done, bf16[2304,512]{1,0:T(8,128)(2,1)} %all-gather.11.cloned.1.call-done), kind=kOutput, calls=%fused_computation.86 | convolution fusion | flops 1207959552 | bytes 5767168 | tf_op jit(solution)/shard_map/dot_general | solution.py:100
  128.6 1.6 reshape.112
  130.2 0.6 fusion.55
  130.8 0.3 subtract_convert_fusion.3
  131.2 0.3 pad_maximum_fusion.2
  131.5 0.2 broadcast_in_dim.12
  131.7 1.0 copy-done.4
  132.7 2.0 fusion.28
  134.7 29.7 %all-gather.9.cloned.1.call-done = bf16[2304,1024]{1,0:T(8,128)(2,1)} async-done(((bf16[288,1024]{1,0:T(8,128)(2,1)}), bf16[2304,1024]{1,0:T(8,128)(2,1)}) %all-gather.9.cloned.1.call-update) | async-done | bytes 4718608 | tf_op jit(solution)/shard_map/all_gather | solution.py:95
  164.5 5.3 %convolution_bitcast_fusion = f32[64,8,8,128]{3,1,2,0:T(8,128)S(1)} fusion(bf16[512,2304]{1,0:T(8,128)(2,1)} %all-gather.5.cloned.1.call-done, bf16[2304,1024]{1,0:T(8,128)(2,1)} %all-gather.9.cloned.1.call-done), kind=kOutput, calls=%fused_computation.22 | convolution fusion | flops 2415919104 | bytes 9175040 | tf_op jit(solution)/shard_map/dot_general | solution.py:100
  169.8 0.5 copy.60
  170.3 0.7 fusion.53
  171.0 0.9 subtract_convert_fusion.1
  171.9 0.2 broadcast_in_dim.18
  172.1 2.7 fusion.12
  174.9 7.5 %fusion.25 = f32[8,8,128,64]{2,3,1,0:T(8,128)} fusion(f32[8,8,64,64]{3,2,1,0:T(8,128)} %fusion.28, f32[8,8,64,64]{2,3,1,0:T(8,128)} %get-tuple-element.25, bf16[8,64,8,64]{3,1,2,0:T(8,128)(2,1)} %copy-done.8, bf16[8,64,8,64]{3,1,2,0:T(8,128)(2,1)S(1)} %get-tuple-element.8, f32[8,8,64]{2,1,0:T(8,128)S(1)} %get-tuple-element.24, ...), kind=kOutput, calls=%fused_computation.52 | convolution fusion | flops 73404480 | bytes 5263360 | tf_op jit(solution)/shard_map/vmap(hqk,qhd->khd)/dot_general | solution.py:65
  182.4 5.8 %convolution_bitcast_fusion.1 = f32[8,64,8,128]{3,1,2,0:T(8,128)S(1)} fusion(bf16[8,64,8,128]{3,1,2,0:T(8,128)(2,1)} %bitcast.91, f32[8,8,64,64]{3,2,1,0:T(8,128)} %fusion.28, f32[8,8,64,64]{2,3,1,0:T(8,128)} %get-tuple-element.25, f32[8,8,64]{2,1,0:T(8,128)S(1)} %get-tuple-element.24, pred[64,64]{0,1:T(8,128)(4,1)S(1)} %iota_compare_fusion), kind=kOutput, calls=%fused_computation.23 | convolution fusion | flops 71307328 | bytes 5263360 | tf_op jit(solution)/shard_map/vmap(hqk,khd->qhd)/dot_general | solution.py:64
  188.2 3.7 %fusion.26 = f32[8,8,64,128]{3,2,1,0:T(8,128)} fusion(bf16[8,64,8,128]{3,2,1,0:T(8,128)(2,1)S(1)} %bitcast.87, f32[8,8,64,64]{2,3,1,0:T(8,128)} %get-tuple-element.25, f32[8,8,64]{2,1,0:T(8,128)S(1)} %get-tuple-element.24, pred[64,64]{0,1:T(8,128)(4,1)S(1)} %iota_compare_fusion), kind=kOutput, calls=%fused_computation.53 | convolution fusion | flops 68419584 | bytes 4214784 | tf_op jit(solution)/shard_map/vmap(hqk,qhd->khd)/dot_general | solution.py:66
  191.9 1.9 reduce_sum.66
  193.8 2.7 reduce_sum.67
  196.5 1.5 copy.53
  197.9 0.4 add_convert_fusion.2
  198.4 0.8 add_convert_fusion
  199.2 0.6 pad_maximum_fusion.1
  199.8 0.9 copy.50
  200.7 0.3 pad_maximum_fusion.3
  201.0 0.4 copy.51
  201.5 2.7 fusion.46
  204.2 1.4 convolution_add_fusion.1
  205.6 0.2 copy-done.6
  205.8 2.9 fusion.1
  208.7 0.0 reduce-scatter.5.cloned.1.call-start
  208.8 0.3 copy.85
  209.0 0.7 copy-done.3
  209.7 0.1 copy_bitcast_fusion.2
  209.9 0.7 copy-done.12
  210.5 7.8 %convolution_convert_fusion = bf16[2304,2048]{1,0:T(8,128)(2,1)} fusion(bf16[512,2304]{1,0:T(8,128)(2,1)S(1)} %copy-done.12, bf16[512,512]{1,0:T(8,128)(2,1)S(1)} %get-tuple-element.26, bf16[512,512]{1,0:T(8,128)(2,1)S(1)} %get-tuple-element.27, bf16[512,1024]{1,0:T(8,128)(2,1)S(1)} %bitcast.94), kind=kOutput, calls=%fused_computation.1 | convolution fusion | flops 4842848256 | bytes 13893632 | tf_op jit(solution)/shard_map/dot_general | solution.py:142
  218.4 1.2 copy-done.5
  219.6 0.7 copy-done.13
  220.3 0.9 fusion.17
  221.1 0.7 copy.47
  221.8 1.2 copy.86
  223.1 33.5 %reduce-scatter.3.cloned.1.call-done = bf16[128,2304]{1,0:T(8,128)(2,1)} async-done(((bf16[512,2304]{1,0:T(8,128)(2,1)}), bf16[128,2304]{1,0:T(8,128)(2,1)}) %reduce-scatter.3.cloned.1.call-update) | async-done | bytes 589840 | tf_op jit(solution)/shard_map/reduce_scatter | solution.py:164
  256.6 1.5 fusion.23
  258.1 40.3 %psum.7 = f32[2304]{0:T(1024)} all-reduce(f32[2304]{0:T(1024)S(1)} %get-tuple-element.6), channel_id=1, replica_groups=mesh['dp'=8,'tensor'=4] {'dp','tensor'}, use_global_device_ids=true, to_apply=%region_9.10 | all-reduce | flops 2304 | bytes 18432 | tf_op jit(solution)/shard_map/psum | solution.py:172
  298.4 2.3 fusion.19
  300.7 36.1 %reduce-scatter.5.cloned.1.call-done = bf16[288,2048]{1,0:T(8,128)(2,1)} async-done(((bf16[2304,2048]{1,0:T(8,128)(2,1)}), bf16[288,2048]{1,0:T(8,128)(2,1)}) %reduce-scatter.5.cloned.1.call-update) | async-done | bytes 1179664 | tf_op jit(solution)/shard_map/reduce_scatter | solution.py:141
  336.7 2.3 slice.52
  339.0 1.2 fusion.54
  (37 shorter events, 0.3 us)
Async XLA Ops:
  7.2 5.6 %copy-start.10 = (bf16[512,1024]{1,0:T(8,128)(2,1)S(1)}, bf16[512,1024]{1,0:T(8,128)(2,1)}, u32[]{:S(2)}) copy-start(bf16[512,1024]{1,0:T(8,128)(2,1)} %param.7) | copy-start | bytes 3145732
  7.2 56.4 %all-gather.5.cloned.1.call-start = ((), (), s32[]{:S(2)}) async-start(), calls=%async_computation.2 | async-start | bytes 2949120 | tf_op jit(solution)/shard_map/all_gather | solution.py:88
  10.7 82.4 %all-gather.7.cloned.1.call-start = ((), (), s32[]{:S(2)}) async-start(), calls=%async_computation.3 | async-start | bytes 2654208 | tf_op jit(solution)/shard_map/all_gather | solution.py:97
  11.4 112.5 %all-gather.11.cloned.1.call-start = ((), (), s32[]{:S(2)}) async-start(), calls=%async_computation.5 | async-start | bytes 2654208 | tf_op jit(solution)/shard_map/all_gather | solution.py:96
  12.2 152.3 %all-gather.9.cloned.1.call-start = ((), (), s32[]{:S(2)}) async-start(), calls=%async_computation.4 | async-start | bytes 5308416 | tf_op jit(solution)/shard_map/all_gather | solution.py:95
  12.8 243.8 %reduce-scatter.3.cloned.1.call-start = ((), (), s32[]{:S(2)}) async-start(), calls=%async_computation.6 | async-start | bytes 2949120 | tf_op jit(solution)/shard_map/reduce_scatter | solution.py:164
  131.7 1.0 copy-start.4
  171.9 3.0 copy-start.8
  172.1 2.8 copy-start.9
  197.9 7.7 %copy-start.2 = (bf16[8,64,4,128]{3,2,1,0:T(4,128)(2,1)}, bf16[8,64,4,128]{3,2,1,0:T(4,128)(2,1)S(1)}, u32[]{:S(2)}) copy-start(bf16[8,64,4,128]{3,2,1,0:T(4,128)(2,1)S(1)} %copy.53) | copy-start | bytes 1572868
  198.4 3.1 slice-start
  199.2 2.3 slice-start.1
  201.5 2.7 copy-start.7
  204.2 1.7 copy-start.6
  208.7 1.0 copy-start.3
  208.7 128.0 %reduce-scatter.5.cloned.1.call-start = ((), (), s32[]{:S(2)}) async-start(), calls=%async_computation.7 | async-start | bytes 10616832 | tf_op jit(solution)/shard_map/reduce_scatter | solution.py:141
  208.7 1.8 copy-start.12
  218.3 1.2 copy-start.5
  218.3 1.9 copy-start.13
  221.1 35.5 %copy-start = (bf16[128,2304]{1,0:T(8,128)(2,1)S(1)}, bf16[128,2304]{1,0:T(8,128)(2,1)}, u32[]{:S(2)}) copy-start(bf16[128,2304]{1,0:T(8,128)(2,1)} %param.6) | copy-start | bytes 1769476
  221.1 35.4 %copy-start.11 = (f32[2304]{0:T(1024)S(1)}, f32[2304]{0:T(1024)}, u32[]{:S(2)}) copy-start(f32[2304]{0:T(1024)} %param.8) | copy-start | bytes 27652
  336.7 2.3 copy-start.1
Sparse Core Ops, SparseCore 0:
  10.8 52.6 all-gather.4
  65.4 27.6 all-gather.6
  95.0 28.8 all-gather.10
  125.7 38.7 all-gather.8
  208.8 47.6 reduce-scatter.2
  259.9 76.7 reduce-scatter.4
where the time goes:
time: 348 us; the launch traced here: 347 us
  waiting for transfers between devices  208 us (60%)
  matrix products  51.2 us (15%)
  blocking collectives  40.3 us (12%)
  local copies, waits for them, and re-layouts  17.4 us (5%)
  other arithmetic  15.6 us (4%)
  between operations  14.5 us (4%)
    all_gather x1, waiting for transfers between devices, per_device(): gathered = lax.all_gather(normed_input, 'tensor', axis=0, tiled=True)  50.3 us
    psum x1, blocking collectives, per_device(): grad_pre = lax.psum(pre_part, ('dp', 'tensor'))  40.3 us
    reduce_scatter x1, waiting for transfers between devices, per_device(): lax.psum_scatter(lax.dot_general(block, joined, contract_first, preferred...  36.1 us
    reduce_scatter x1, waiting for transfers between devices, per_device(): lax.psum_scatter(total.astype(jnp.bfloat16), 'tensor', scatter_dimension=...  33.5 us
    all_gather x1, waiting for transfers between devices, per_device(): lax.all_gather(w_query, 'dp', axis=0, tiled=True)  29.7 us
    all_gather x1, waiting for transfers between devices, per_device(): lax.all_gather(value_weight, 'dp', axis=0, tiled=True)  29.6 us
    all_gather x1, waiting for transfers between devices, per_device(): lax.all_gather(key_weight, 'dp', axis=0, tiled=True)  26.8 us
    dot_general x3, matrix products, per_device(): jnp.dot(gathered, piece, preferred_element_type=jnp.float32)  13.8 us
  transfers between devices with their start and end apart: 6, of which 6 were waited for; matrix products, arithmetic and copies ran while one was open for 8% of the time, Pallas kernels for 0%

commit v1 on v0

--- a/solution.py
+++ b/solution.py
@@ -85,7 +85,14 @@
     inv_one = lax.rsqrt(jnp.mean(rows_f * rows_f, -1, keepdims=True) + EPS)
     unit_one = rows_f * inv_one
     normed_input = (unit_one * pre_gain).astype(jnp.bfloat16)
-    gathered = lax.all_gather(normed_input, "tensor", axis=0, tiled=True)
+    ring = [normed_input]
+    for hop in range(3):
+        ring.append(lax.ppermute(ring[-1], "tensor", [(dev, (dev + 1) % 4) for dev in range(4)]))
+    gathered = jnp.roll(
+        jnp.concatenate(ring[::-1], axis=0),
+        (lax.axis_index("tensor") + 1) * ring[0].shape[0],
+        axis=0,
+    )
     segment_length = gathered.shape[0]
     token_span = SEQ_LEN
     pieces_count = segment_length // token_span

time: 348 us -> 296 us (0.85)
  waiting for transfers between devices: 208 us -> 145 us
  matrix products: 51.2 us -> 55.4 us
  local copies, waits for them, and re-layouts: 17.4 us -> 21.4 us
    all_gather x1 -> x0, waiting for transfers between devices: 50.3 us -> none  [per_device(): gathered = lax.all_gather(normed_input, 'tensor', axis=0, tiled=True)]
    ppermute x0 -> x3, waiting for transfers between devices: none -> 45.4 us  [per_device(): lax.ppermute(ring[-1], 'tensor', [(dev, (dev + 1) % 4) for dev in range(4)])]
    all_gather x1, waiting for transfers between devices: 29.6 us -> 0.01 us  [per_device(): lax.all_gather(value_weight, 'dp', axis=0, tiled=True)]
    all_gather x1, waiting for transfers between devices: 26.8 us -> 0.02 us  [per_device(): lax.all_gather(key_weight, 'dp', axis=0, tiled=True)]
    unnamed x36 -> x34, local copies, waits for them, and re-layouts: 6.72 us -> 11.8 us
  transfers between devices with their start and end apart: 6 -> 8, of which waited for: 6 -> 6; matrix products, arithmetic and copies ran while one was open for 8% -> 15% of each run, Pallas kernels for 0% -> 0%
where the time goes in v1:
time: 296 us; the launch traced here: 295 us
  waiting for transfers between devices  145 us (49%)
  matrix products  55.4 us (19%)
  blocking collectives  40.3 us (14%)
  local copies, waits for them, and re-layouts  21.4 us (7%)
  other arithmetic  15.5 us (5%)
  between operations  14.1 us (5%)
  starting transfers between devices  3.3 us (1%)
    ppermute x3, waiting for transfers between devices, per_device(): lax.ppermute(ring[-1], 'tensor', [(dev, (dev + 1) % 4) for dev in range(4)])  45.4 us
    psum x1, blocking collectives, per_device(): grad_pre = lax.psum(pre_part, ('dp', 'tensor'))  40.3 us
    reduce_scatter x1, waiting for transfers between devices, per_device(): lax.psum_scatter(lax.dot_general(block, joined, contract_first, preferred...  36.1 us
    reduce_scatter x1, waiting for transfers between devices, per_device(): lax.psum_scatter(total.astype(jnp.bfloat16), 'tensor', scatter_dimension=...  32.4 us
    all_gather x1, waiting for transfers between devices, per_device(): lax.all_gather(w_query, 'dp', axis=0, tiled=True)  29.1 us
    dot_general x3, matrix products, per_device(): jnp.dot(gathered, piece, preferred_element_type=jnp.float32)  13.9 us
    unnamed x34, local copies, waits for them, and re-layouts  11.8 us
    dot_general x1, matrix products, per_device(): lax.dot_general(block, joined, contract_first, preferred_element_type=jnp...  9.4 us
  transfers between devices with their start and end apart: 8, of which 6 were waited for; matrix products, arithmetic and copies ran while one was open for 15% of the time, Pallas kernels for 0%

profile of v1, /device:TPU:0, one launch (start us, length us, event | category | flops | bytes accessed | tf_op | source)
XLA Modules:
  0.0 295.0 jit_solution(13423654210083702763)
XLA Ops:
  7.2 0.7 all-gather.4.cloned.1.call-update
  8.0 0.7 all-gather.8.cloned.1.call-update
  8.7 0.7 all-gather.6.cloned.1.call-update
  9.4 1.3 fusion.31
  10.7 0.9 fusion.29
  11.6 3.1 %collective-permute-start = (bf16[128,2304]{1,0:T(8,128)(2,1)S(1)}, bf16[128,2304]{1,0:T(8,128)(2,1)S(1)}, u32[]{:S(2)}, u32[]{:S(2)}) collective-permute-start(bf16[128,2304]{1,0:T(8,128)(2,1)S(1)} %fusion.29), channel_id=1, source_target_pairs={{0,1},{1,2},{2,3},{3,0},{4,5},{5,6},{6,7},{7,4},{8,9},{9,10},{10,1... | collective-permute-start | bytes 1769480 | tf_op jit(solution)/shard_map/ppermute | solution.py:90
  14.7 15.4 %collective-permute-done = bf16[128,2304]{1,0:T(8,128)(2,1)S(1)} collective-permute-done((bf16[128,2304]{1,0:T(8,128)(2,1)S(1)}, bf16[128,2304]{1,0:T(8,128)(2,1)S(1)}, u32[]{:S(2)}, u32[]{:S(2)}) %collective-permute-start) | collective-permute-done | bytes 589856 | tf_op jit(solution)/shard_map/ppermute | solution.py:90
  30.1 16.3 %collective-permute-done.1 = bf16[128,2304]{1,0:T(8,128)(2,1)S(1)} collective-permute-done((bf16[128,2304]{1,0:T(8,128)(2,1)S(1)}, bf16[128,2304]{1,0:T(8,128)(2,1)S(1)}, u32[]{:S(2)}, u32[]{:S(2)}) %collective-permute-start.1) | collective-permute-done | bytes 589856 | tf_op jit(solution)/shard_map/ppermute | solution.py:90
  46.4 1.5 copy.62
  48.1 13.7 %collective-permute-done.2 = bf16[128,2304]{1,0:T(8,128)(2,1)S(1)} collective-permute-done((bf16[128,2304]{1,0:T(8,128)(2,1)S(1)}, bf16[128,2304]{1,0:T(8,128)(2,1)S(1)}, u32[]{:S(2)}, u32[]{:S(2)}) %collective-permute-start.2) | collective-permute-done | bytes 589856 | tf_op jit(solution)/shard_map/ppermute | solution.py:90
  61.8 0.8 constant_dynamic-update-slice_fusion.7
  62.7 0.9 constant_dynamic-update-slice_fusion.6
  63.5 0.9 constant_dynamic-update-slice_fusion.5
  64.4 1.0 constant_dynamic-update-slice_fusion.4
  65.4 0.9 constant_dynamic-update-slice_fusion.3
  66.3 0.8 constant_dynamic-update-slice_fusion.2
  67.2 0.9 constant_dynamic-update-slice_fusion.1
  68.0 1.0 constant_dynamic-update-slice_fusion
  69.0 3.8 %fusion.24 = bf16[512,512]{1,0:T(8,128)(2,1)S(1)} fusion(bf16[2304,512]{1,0:T(8,128)(2,1)} %all-gather.4.cloned.1.call-done, bf16[1024,2304]{1,0:T(8,128)(2,1)} %constant_dynamic-update-slice_fusion, s32[]{:T(128)S(6)} %select_n.18), kind=kOutput, calls=%fused_computation.42 | convolution fusion | flops 1208221696 | bytes 5242884 | tf_op jit(solution)/shard_map/dot_general | solution.py:107
  73.1 4.7 %fusion.12 = f32[512,512]{1,0:T(8,128)} fusion(bf16[2304,512]{1,0:T(8,128)(2,1)} %all-gather.8.cloned.1.call-done, bf16[1024,2304]{1,0:T(8,128)(2,1)} %constant_dynamic-update-slice_fusion, s32[]{:T(128)S(6)} %select_n.18), kind=kOutput, calls=%fused_computation.25 | convolution fusion | flops 1207959552 | bytes 5767172 | tf_op jit(solution)/shard_map/dot_general | solution.py:107
  77.9 1.6 reshape.112
  79.4 0.6 fusion.68
  80.1 0.3 subtract_convert_fusion.3
  80.4 0.3 pad_maximum_fusion.2
  80.7 0.2 broadcast_in_dim.12
  81.0 1.0 copy-done.3
  81.9 2.0 fusion.37
  83.9 29.1 %all-gather.6.cloned.1.call-done = bf16[2304,1024]{1,0:T(8,128)(2,1)} async-done(((bf16[288,1024]{1,0:T(8,128)(2,1)}), bf16[2304,1024]{1,0:T(8,128)(2,1)}) %all-gather.6.cloned.1.call-update) | async-done | bytes 4718608 | tf_op jit(solution)/shard_map/all_gather | solution.py:102
  113.0 5.3 %convolution_bitcast_fusion = f32[64,8,8,128]{3,1,2,0:T(8,128)S(1)} fusion(bf16[2304,1024]{1,0:T(8,128)(2,1)} %all-gather.6.cloned.1.call-done, bf16[1024,2304]{1,0:T(8,128)(2,1)} %constant_dynamic-update-slice_fusion, s32[]{:T(128)S(6)} %select_n.18), kind=kOutput, calls=%fused_computation.22 | convolution fusion | flops 2415919104 | bytes 9175044 | tf_op jit(solution)/shard_map/dot_general | solution.py:107
  118.4 0.5 copy.60
  118.8 0.7 fusion.66
  119.5 0.9 subtract_convert_fusion.1
  120.4 0.2 broadcast_in_dim.18
  120.7 2.6 fusion.18
  123.3 7.3 %fusion.34 = f32[8,8,128,64]{2,3,1,0:T(8,128)} fusion(f32[8,8,64,64]{3,2,1,0:T(8,128)} %fusion.37, f32[8,8,64,64]{2,3,1,0:T(8,128)} %get-tuple-element.25, bf16[8,64,8,64]{3,1,2,0:T(8,128)(2,1)} %copy-done.7, bf16[8,64,8,64]{3,1,2,0:T(8,128)(2,1)S(1)} %get-tuple-element.8, f32[8,8,64]{2,1,0:T(8,128)S(1)} %get-tuple-element.24, ...), kind=kOutput, calls=%fused_computation.58 | convolution fusion | flops 73404480 | bytes 5263360 | tf_op jit(solution)/shard_map/vmap(hqk,qhd->khd)/dot_general | solution.py:65
  130.6 7.0 %convolution_bitcast_fusion.1 = f32[8,64,8,128]{3,1,2,0:T(8,128)} fusion(bf16[8,64,8,128]{3,1,2,0:T(8,128)(2,1)} %bitcast.87, f32[8,8,64,64]{3,2,1,0:T(8,128)} %fusion.37, f32[8,8,64,64]{2,3,1,0:T(8,128)} %get-tuple-element.25, f32[8,8,64]{2,1,0:T(8,128)S(1)} %get-tuple-element.24, pred[64,64]{0,1:T(8,128)(4,1)S(1)} %iota_compare_fusion), kind=kOutput, calls=%fused_computation.23 | convolution fusion | flops 71307328 | bytes 5263360 | tf_op jit(solution)/shard_map/vmap(hqk,khd->qhd)/dot_general | solution.py:64
  137.7 3.7 %fusion.35 = f32[8,8,64,128]{3,2,1,0:T(8,128)} fusion(bf16[8,64,8,128]{3,2,1,0:T(8,128)(2,1)S(1)} %bitcast.83, f32[8,8,64,64]{2,3,1,0:T(8,128)} %get-tuple-element.25, f32[8,8,64]{2,1,0:T(8,128)S(1)} %get-tuple-element.24, pred[64,64]{0,1:T(8,128)(4,1)S(1)} %iota_compare_fusion), kind=kOutput, calls=%fused_computation.59 | convolution fusion | flops 68419584 | bytes 4214784 | tf_op jit(solution)/shard_map/vmap(hqk,qhd->khd)/dot_general | solution.py:66
  141.3 1.9 reduce_sum.66
  143.2 1.8 reduce_sum.67
  145.0 0.4 copy.53
  145.4 0.4 add_convert_fusion.2
  145.9 0.7 copy-done.1
  146.6 0.8 add_convert_fusion
  147.4 0.6 pad_maximum_fusion.1
  148.0 0.9 copy.50
  148.9 0.3 pad_maximum_fusion.3
  149.2 0.4 copy.51
  149.7 2.7 fusion.59
  152.4 1.4 convolution_add_fusion.1
  153.8 0.2 copy-done.5
  154.0 2.9 fusion.1
  157.0 0.3 copy.85
  157.4 9.4 %convolution_convert_fusion = bf16[2304,2048]{1,0:T(8,128)(2,1)} fusion(bf16[512,512]{1,0:T(8,128)(2,1)S(1)} %get-tuple-element.26, bf16[512,512]{1,0:T(8,128)(2,1)S(1)} %get-tuple-element.27, bf16[512,1024]{1,0:T(8,128)(2,1)S(1)} %bitcast.90, bf16[1024,2304]{1,0:T(8,128)(2,1)} %constant_dynamic-update-slice_fusion, s32[]{:T(128)S(6)} %select_n.18), kind=kOutput, calls=%fused_computation.1 | convolution fusion | flops 4842848256 | bytes 13893636 | tf_op jit(solution)/shard_map/dot_general | solution.py:149
  166.9 1.2 copy-done.4
  168.1 2.4 fusion.23
  170.5 0.7 copy.47
  171.2 1.2 copy.86
  172.5 32.4 %reduce-scatter.3.cloned.1.call-done = bf16[128,2304]{1,0:T(8,128)(2,1)} async-done(((bf16[512,2304]{1,0:T(8,128)(2,1)}), bf16[128,2304]{1,0:T(8,128)(2,1)}) %reduce-scatter.3.cloned.1.call-update) | async-done | bytes 589840 | tf_op jit(solution)/shard_map/reduce_scatter | solution.py:171
  204.8 1.5 fusion.32
  206.3 40.3 %psum.7 = f32[2304]{0:T(1024)} all-reduce(f32[2304]{0:T(1024)S(1)} %get-tuple-element.6), channel_id=1, replica_groups=mesh['dp'=8,'tensor'=4] {'dp','tensor'}, use_global_device_ids=true, to_apply=%region_9.10 | all-reduce | flops 2304 | bytes 18432 | tf_op jit(solution)/shard_map/psum | solution.py:179
  246.6 2.3 fusion.28
  248.9 36.1 %reduce-scatter.5.cloned.1.call-done = bf16[288,2048]{1,0:T(8,128)(2,1)} async-done(((bf16[2304,2048]{1,0:T(8,128)(2,1)}), bf16[288,2048]{1,0:T(8,128)(2,1)}) %reduce-scatter.5.cloned.1.call-update) | async-done | bytes 1179664 | tf_op jit(solution)/shard_map/reduce_scatter | solution.py:148
  285.0 2.3 slice.52
  287.3 1.2 fusion.67
  (40 shorter events, 0.9 us)
Async XLA Ops:
  7.2 3.6 %copy-start = (bf16[128,2304]{1,0:T(8,128)(2,1)S(1)}, bf16[128,2304]{1,0:T(8,128)(2,1)}, u32[]{:S(2)}) copy-start(bf16[128,2304]{1,0:T(8,128)(2,1)} %param.6) | copy-start | bytes 1769476
  7.2 61.9 %all-gather.4.cloned.1.call-start = ((), (), s32[]{:S(2)}) async-start(), calls=%async_computation.2 | async-start | bytes 2654208 | tf_op jit(solution)/shard_map/all_gather | solution.py:104
  7.9 65.2 %all-gather.8.cloned.1.call-start = ((), (), s32[]{:S(2)}) async-start(), calls=%async_computation.4 | async-start | bytes 2654208 | tf_op jit(solution)/shard_map/all_gather | solution.py:103
  8.7 104.4 %all-gather.6.cloned.1.call-start = ((), (), s32[]{:S(2)}) async-start(), calls=%async_computation.3 | async-start | bytes 5308416 | tf_op jit(solution)/shard_map/all_gather | solution.py:102
  9.4 195.4 %reduce-scatter.3.cloned.1.call-start = ((), (), s32[]{:S(2)}) async-start(), calls=%async_computation.5 | async-start | bytes 2949120 | tf_op jit(solution)/shard_map/reduce_scatter | solution.py:171
  11.6 18.5 %collective-permute-start = (bf16[128,2304]{1,0:T(8,128)(2,1)S(1)}, bf16[128,2304]{1,0:T(8,128)(2,1)S(1)}, u32[]{:S(2)}, u32[]{:S(2)}) collective-permute-start(bf16[128,2304]{1,0:T(8,128)(2,1)S(1)} %fusion.29), channel_id=1, source_target_pairs={{0,1},{1,2},{2,3},{3,0},{4,5},{5,6},{6,7},{7,4},{8,9},{9,10},{10,1... | collective-permute-start | bytes 1769480 | tf_op jit(solution)/shard_map/ppermute | solution.py:90
  30.1 16.3 %collective-permute-start.1 = (bf16[128,2304]{1,0:T(8,128)(2,1)S(1)}, bf16[128,2304]{1,0:T(8,128)(2,1)S(1)}, u32[]{:S(2)}, u32[]{:S(2)}) collective-permute-start(bf16[128,2304]{1,0:T(8,128)(2,1)S(1)} %collective-permute-done), channel_id=1, source_target_pairs={{0,1},{1,2},{2,3},{3,0},{4,5},{5,6},{6,7},{7,4},{8,9},{9,10},{10,1... | collective-permute-start | bytes 1769480 | tf_op jit(solution)/shard_map/ppermute | solution.py:90
  46.4 15.4 %collective-permute-start.2 = (bf16[128,2304]{1,0:T(8,128)(2,1)S(1)}, bf16[128,2304]{1,0:T(8,128)(2,1)S(1)}, u32[]{:S(2)}, u32[]{:S(2)}) collective-permute-start(bf16[128,2304]{1,0:T(8,128)(2,1)S(1)} %collective-permute-done.1), channel_id=1, source_target_pairs={{0,1},{1,2},{2,3},{3,0},{4,5},{5,6},{6,7},{7,4},{8,9},{9,10},{10,1... | collective-permute-start | bytes 1769480 | tf_op jit(solution)/shard_map/ppermute | solution.py:90
  47.9 16.5 %copy-start.9 = (f32[2304]{0:T(1024)S(1)}, f32[2304]{0:T(1024)}, u32[]{:S(2)}) copy-start(f32[2304]{0:T(1024)} %param.8) | copy-start | bytes 27652
  81.0 1.0 copy-start.3
  120.4 2.9 copy-start.7
  120.7 2.7 copy-start.8
  145.0 1.6 copy-start.1
  146.6 3.1 %slice-start = ((s8[4718592]{0:T(1024)(128)(4,1)}), s8[4194304]{0:T(1024)(128)(4,1)S(1)}, s32[]{:S(2)}) async-start(s8[4718592]{0:T(1024)(128)(4,1)} %bitcast.91), calls=%async_computation.7 | async-start | bytes 8388608
  147.4 2.3 slice-start.1
  149.7 2.7 copy-start.6
  152.4 1.7 copy-start.5
  157.0 128.1 %reduce-scatter.5.cloned.1.call-start = ((), (), s32[]{:S(2)}) async-start(), calls=%async_computation.6 | async-start | bytes 10616832 | tf_op jit(solution)/shard_map/reduce_scatter | solution.py:148
  166.8 1.2 copy-start.4
  285.0 2.3 copy-start.2
Sparse Core Ops, SparseCore 0:
  9.9 31.5 all-gather.3
  43.4 28.8 all-gather.7
  74.2 38.7 all-gather.5
  157.1 47.6 reduce-scatter.2
  208.2 76.8 reduce-scatter.4
